TPU v7x, 32 devices: a whole 2x2x4 slice. The times are simulated.
32 devices in a mesh: fsdp: 4 (over z), ctx: 4 (over y, x), tp: 2 (over core).
Axes of the slice: x: 2, y: 2, z: 4, core: 2. Of those that a mesh axis runs over, the one named last changes fastest.
Arguments:
- block_input: bfloat16 [4, 1024, 1600], P('fsdp', 'ctx'), may hold values from -8 to 8
- segments: int32 [4, 1024], P('fsdp', 'ctx'), may hold values from 0 to 3, never falling along the last dimension, each value on 1 to 512 neighbouring positions
- ln1_gain: float32 [1600], replicated, may hold values from 0.5 to 1.5
- ln1_shift: float32 [1600], replicated, may hold values from -3 to 3
- qkv_weight: bfloat16 [1600, 4800], P('fsdp'), may hold values from -4 to 4
- out_weight: bfloat16 [1600, 1600], P(None, 'fsdp'), may hold values from -0.4375 to 0.4375
- ln2_gain: float32 [1600], replicated, may hold values from 0.5 to 1.5
- ln2_shift: float32 [1600], replicated, may hold values from -3 to 3
- fc_weight: bfloat16 [1600, 6400], P('fsdp', 'tp'), may hold values from -0.15625 to 0.15625
- proj_weight: bfloat16 [6400, 1600], P('tp', 'fsdp'), may hold values from -0.078125 to 0.078125
- cotangent: bfloat16 [4, 1024, 1600], P('fsdp', 'ctx'), may hold values from -6 to 6
Outputs:
- block_output: bfloat16 [4, 1024, 1600], P('fsdp', 'ctx')
- grad_input: float32 [4, 1024, 1600], P('fsdp', 'ctx')
- grad_ln1_gain: float32 [1600], P(('fsdp', 'ctx'))
- grad_ln1_shift: float32 [1600], P(('fsdp', 'ctx'))
- grad_qkv_weight: float32 [1600, 4800], P(('fsdp', 'ctx'))
- grad_out_weight: float32 [1600, 1600], P(None, ('fsdp', 'ctx'))
- grad_ln2_gain: float32 [1600], P(('fsdp', 'ctx'))
- grad_ln2_shift: float32 [1600], P(('fsdp', 'ctx'))
- grad_fc_weight: float32 [1600, 6400], P(('fsdp', 'ctx'), 'tp')
- grad_proj_weight: float32 [6400, 1600], P('tp', ('fsdp', 'ctx'))
All inputs are finite; a program needn't handle non-finite values.
Results may differ from a plain program's by a relative error of at most 0.013.
The roundings to bfloat16 on the way count: a program that leaves them out, or rounds other values in their place, can miss the bound.
Values may be sent and summed in bfloat16 or wider, within the bound.
A program may use at most 320 MiB of HBM per device.

v0:
```python
import jax
import jax.numpy as jnp
from jax import lax
from jax.sharding import PartitionSpec as P

H = 25
HD = 64
EPS = 1e-05
BF = jnp.bfloat16
F32 = jnp.float32
PLANE = ("ctx", "tp")


def dot(lhs, rhs, dims):
    return lax.dot_general(lhs, rhs, (dims, ((), ())), preferred_element_type=F32)


def moments(values):
    centered = values - jnp.mean(values, axis=-1, keepdims=True)
    inv_std = lax.rsqrt(jnp.mean(centered * centered, axis=-1, keepdims=True) + EPS)
    return (centered * inv_std, inv_std)


def norm_back(upstream, normed, inv_std, gain):
    scaled = upstream * gain
    return inv_std * (
        scaled
        - jnp.mean(scaled, axis=-1, keepdims=True)
        - normed * jnp.mean(scaled * normed, axis=-1, keepdims=True)
    )


def gelu_tanh(values):
    return jax.nn.gelu(values, approximate=True)


def masked_scores(queries, keys, seg):
    length = queries.shape[0]
    scores = jnp.einsum("qhd,khd->hqk", queries, keys, preferred_element_type=F32) * HD ** (-0.5)
    pos = jnp.arange(length, dtype=jnp.int32)
    allowed = (pos[None, :] <= pos[:, None]) & (seg[None, :] == seg[:, None])
    return jnp.where(allowed[None], scores, -1e30)


def attend(queries, keys, values, seg):
    scores = masked_scores(queries, keys, seg)
    row_max = jnp.max(scores, axis=-1, keepdims=True)
    exponent = jnp.exp(scores - row_max)
    total = jnp.sum(exponent, axis=-1, keepdims=True)
    probs = (exponent / total).astype(BF)
    attended = jnp.einsum("hqk,khd->qhd", probs, values, preferred_element_type=F32)
    return (attended.astype(BF), row_max + jnp.log(total))


def attend_back(queries, keys, values, seg, lse, grad):
    probs = jnp.exp(masked_scores(queries, keys, seg) - lse)
    grad_v = jnp.einsum("hqk,qhd->khd", probs.astype(BF), grad, preferred_element_type=F32)
    grad_p = jnp.einsum("qhd,khd->hqk", grad, values, preferred_element_type=F32)
    inner = jnp.sum(probs * grad_p, axis=-1, keepdims=True)
    raw = (probs * (grad_p - inner) * HD ** (-0.5)).astype(BF)
    grad_q = jnp.einsum("hqk,khd->qhd", raw, keys, preferred_element_type=F32)
    grad_k = jnp.einsum("hqk,qhd->khd", raw, queries, preferred_element_type=F32)
    return (grad_q, grad_k, grad_v)


def build(mesh):
    ctx_n, tp_n = (mesh.shape["ctx"], mesh.shape["tp"])
    members = ctx_n * tp_n
    slots = -(-H // members)
    starts = [m * H // members for m in range(members + 1)]
    counts = [starts[m + 1] - starts[m] for m in range(members)]
    width = slots * HD

    def local(x, segments, g1, b1, wqkv, wout, g2, b2, wfc, wproj, cot):
        x, cot = (x[0], cot[0])
        rows, model = x.shape
        tp_i, ctx_i = (lax.axis_index("tp"), lax.axis_index("ctx"))
        member = ctx_i * tp_n + tp_i
        own = rows // tp_n
        head0 = member * H // members
        head_n = (member + 1) * H // members - head0
        valid = jnp.arange(width, dtype=jnp.int32) < head_n * HD

        def cols(matrix, start, size):
            return lax.dynamic_slice_in_dim(matrix, start, size, 1)

        def rows_of(matrix, start, size):
            return lax.dynamic_slice_in_dim(matrix, start, size, 0)

        wq = jnp.concatenate([cols(wqkv, p * H * HD + head0 * HD, width) for p in range(3)], axis=1)
        wq = lax.all_gather(wq, "fsdp", axis=0, tiled=True)
        part = model // members
        wo = lax.all_gather(rows_of(wout, member * part, part), "fsdp", axis=1, tiled=True)
        wo = lax.all_gather(wo, PLANE, axis=0, tiled=True)
        hidden = wfc.shape[1] // ctx_n
        wf = lax.all_gather(cols(wfc, ctx_i * hidden, hidden), "fsdp", axis=0, tiled=True)
        wp = lax.all_gather(rows_of(wproj, ctx_i * hidden, hidden), "fsdp", axis=1, tiled=True)

        def to_plane(v):
            return lax.all_gather(v, PLANE, axis=0, tiled=True)

        def from_plane(v):
            return lax.psum_scatter(v, PLANE, scatter_dimension=0, tiled=True)

        x_own = rows_of(x, tp_i * own, own)
        cot_own = rows_of(cot, tp_i * own, own)
        x_all = to_plane(x_own)
        cot_all = to_plane(cot_own)
        seg = lax.all_gather(segments[0], "ctx", axis=0, tiled=True)
        length = x_all.shape[0]
        n1_all, _ = moments(x_all.astype(F32))
        h1 = (n1_all * g1 + b1).astype(BF)
        qkv = dot(h1, wq, ((1,), (0,))).astype(BF).reshape(length, 3, slots, HD)
        q, k, v = (qkv[:, 0], qkv[:, 1], qkv[:, 2])
        attended, lse = attend(q, k, v, seg)
        attended = attended.reshape(length, width)
        spread = lax.all_to_all(attended, PLANE, 0, 1, tiled=True)
        att_own = jnp.concatenate(
            [spread[:, m * width : m * width + counts[m] * HD] for m in range(members)], axis=1
        )
        x_own_f32 = x_own.astype(F32)
        r1 = x_own_f32 + dot(att_own, wo, ((1,), (0,)))
        n2, s2 = moments(r1)
        h2 = to_plane((n2 * g2 + b2).astype(BF))
        pre = dot(h2, wf, ((1,), (0,)))
        act, pull = jax.vjp(gelu_tanh, pre)
        act = act.astype(BF)
        mlp = from_plane(dot(act, wp, ((1,), (0,))))
        out = lax.all_gather((r1 + mlp).astype(BF), "tp", axis=0, tiled=True)
        grad_proj = dot(act, cot_all, ((0,), (0,)))
        grad_pre = pull(dot(cot_all, wp, ((1,), (1,))))[0].astype(BF)
        grad_fc = dot(h2, grad_pre, ((0,), (0,)))
        grad_h2 = from_plane(dot(grad_pre, wf, ((1,), (1,))))
        grad_r1 = cot_own.astype(F32) + norm_back(grad_h2, n2, s2, g2)
        grad_att = to_plane(grad_r1.astype(BF))
        wo_mine = rows_of(wo, head0 * HD, width)
        grad_out = dot(attended, grad_att, ((0,), (0,)))
        grad_attended = jnp.where(valid, dot(grad_att, wo_mine, ((1,), (1,))), 0.0).astype(BF)
        dq, dk, dv = attend_back(q, k, v, seg, lse, grad_attended.reshape(length, slots, HD))
        dqkv = jnp.stack([dq, dk, dv], axis=1).astype(BF).reshape(length, 3 * width)
        grad_qkv = dot(h1, dqkv, ((0,), (0,)))
        grad_h1 = from_plane(dot(dqkv, wq, ((1,), (1,))))
        n1, s1 = moments(x_own_f32)
        grad_x = grad_r1 + norm_back(grad_h1, n1, s1, g1)
        grad_x = lax.all_gather(grad_x, "tp", axis=0, tiled=True)

        def over_fsdp(v, dim):
            return lax.psum_scatter(v, "fsdp", scatter_dimension=dim, tiled=True)

        fc_out = lax.all_to_all(over_fsdp(grad_fc, 0), "ctx", 0, 1, tiled=True)
        proj_out = lax.all_to_all(over_fsdp(grad_proj, 1), "ctx", 1, 0, tiled=True)
        gq = over_fsdp(grad_qkv, 0).astype(BF)
        gq = gq.reshape(ctx_n, gq.shape[0] // ctx_n, 3 * width)
        gq = lax.all_gather(lax.all_to_all(gq, "ctx", 0, 0, tiled=True), "tp", axis=1)
        gq = gq.reshape((members,) + gq.shape[2:])
        qkv_out = jnp.concatenate(
            [
                gq[m][:, p * width : p * width + counts[m] * HD]
                for p in range(3)
                for m in range(members)
            ],
            axis=1,
        ).astype(F32)
        go = over_fsdp(grad_out, 1).astype(BF)
        go = lax.all_to_all(go, "ctx", 1, 0, tiled=True)
        go = lax.all_gather(go.reshape(ctx_n, width, go.shape[1]), "tp", axis=1)
        go = go.reshape((members,) + go.shape[2:])
        out_out = jnp.concatenate([go[m][: counts[m] * HD] for m in range(members)], axis=0)
        out_out = out_out.astype(F32)
        sums = jnp.stack(
            [
                jnp.sum(grad_h1 * n1, axis=0),
                jnp.sum(grad_h1, axis=0),
                jnp.sum(grad_h2 * n2, axis=0),
                jnp.sum(grad_h2, axis=0),
            ]
        )
        sums = lax.psum_scatter(
            lax.psum(sums, "tp"), ("fsdp", "ctx"), scatter_dimension=1, tiled=True
        )
        return (
            out[None],
            grad_x[None],
            sums[0],
            sums[1],
            qkv_out,
            out_out,
            sums[2],
            sums[3],
            fc_out,
            proj_out,
        )

    return local


def solution(mesh):
    placed = (
        P("fsdp", "ctx", None),
        P("fsdp", "ctx"),
        P(),
        P(),
        P("fsdp", None),
        P(None, "fsdp"),
        P(),
        P(),
        P("fsdp", "tp"),
        P("tp", "fsdp"),
        P("fsdp", "ctx", None),
    )
    both = ("fsdp", "ctx")
    return jax.shard_map(
        build(mesh),
        mesh=mesh,
        in_specs=placed,
        out_specs=(
            P("fsdp", "ctx", None),
            P("fsdp", "ctx", None),
            P(both),
            P(both),
            P(both, None),
            P(None, both),
            P(both),
            P(both),
            P(both, "tp"),
            P("tp", both),
        ),
        check_vma=False,
    )
```

profile of v0, /device:TPU:0, one launch (start us, length us, event | category | flops | bytes accessed | tf_op | source)
XLA Modules:
  0.0 1052.5 jit_solution(6024526135875657321)
XLA Ops:
  12.9 21.7 %all_gather.48 = bf16[200,1600]{0,1:T(8,128)(2,1)S(1)} all-gather(bf16[200,400]{0,1:T(8,128)(2,1)S(1)} %constant_dynamic-slice_fusion.3), channel_id=1, replica_groups=mesh['fsdp'=4,'ctx'=4,'tp'=2] {'fsdp'}, dimensions={1}, use_global_device_ids=true | all-gather | bytes 800000 | tf_op jit(solution)/shard_map/all_gather | solution.py:93
  37.0 8.2 all-gather.1
  50.4 50.2 %all-gather.16.cloned.1.call-done = bf16[1600,768]{1,0:T(8,128)(2,1)} async-done(((bf16[400,768]{1,0:T(8,128)(2,1)}), bf16[1600,768]{1,0:T(8,128)(2,1)}) %all-gather.16.cloned.1.call-update) | async-done | bytes 2457616 | tf_op jit(solution)/shard_map/all_gather | solution.py:91
  100.6 6.1 convolution_convert_fusion
  106.8 7.5 fusion.91
  114.3 8.0 fusion.4
  122.3 8.3 fusion.48
  130.7 17.1 %all_to_all.78 = bf16[8,128,256]{1,2,0:T(8,128)(2,1)S(1)} all-to-all(bf16[8,128,256]{1,2,0:T(8,128)(2,1)S(1)} %copy.96), channel_id=1, replica_groups=mesh['fsdp'=4,'ctx'=4,'tp'=2] {'ctx','tp'}, dimensions={0} | all-to-all | bytes 1048576 | tf_op jit(solution)/shard_map/all_to_all | solution.py:117
  157.6 52.0 %all-gather.22.cloned.1.call-done = bf16[1600,800]{1,0:T(8,128)(2,1)} async-done(((bf16[400,800]{1,0:T(8,128)(2,1)}), bf16[1600,800]{1,0:T(8,128)(2,1)}) %all-gather.22.cloned.1.call-update) | async-done | bytes 2560016 | tf_op jit(solution)/shard_map/all_gather | solution.py:96
  209.6 34.3 %all-gather.20.cloned.1.call-done = bf16[1024,1600]{0,1:T(8,128)(2,1)} async-done(((bf16[128,1600]{0,1:T(8,128)(2,1)}), bf16[1024,1600]{0,1:T(8,128)(2,1)}) %all-gather.20.cloned.1.call-update) | async-done | bytes 3276816 | tf_op jit(solution)/shard_map/all_gather | solution.py:100
  243.9 7.6 fusion.93
  251.5 53.2 %all-gather.24.cloned.1.call-done = bf16[800,1600]{0,1:T(8,128)(2,1)} async-done(((bf16[800,400]{0,1:T(8,128)(2,1)}), bf16[800,1600]{0,1:T(8,128)(2,1)}) %all-gather.24.cloned.1.call-update) | async-done | bytes 2560016 | tf_op jit(solution)/shard_map/all_gather | solution.py:97
  304.8 34.5 %all-gather.32.cloned.1.call-done = bf16[1,1024,1600]{1,2,0:T(8,128)(2,1)} async-done(((bf16[1,128,1600]{1,2,0:T(8,128)(2,1)}), bf16[1,1024,1600]{1,2,0:T(8,128)(2,1)}) %all-gather.32.cloned.1.call-update) | async-done | bytes 3276816 | tf_op jit(solution)/shard_map/all_gather | solution.py:100
  339.2 9.0 fusion.31
  349.4 5.5 fusion.96
  354.9 63.0 %reduce-scatter.11.cloned.1.call-done = f32[128,1600]{0,1:T(8,128)} async-done(((f32[1024,1600]{0,1:T(8,128)}), f32[128,1600]{0,1:T(8,128)}) %reduce-scatter.11.cloned.1.call-update) | async-done | bytes 819216 | tf_op jit(solution)/shard_map/reduce_scatter | solution.py:103
  422.0 9.8 reduce-scatter.21.cloned.1.call-start
  431.8 9.1 fusion.32
  441.0 14.4 %all-gather.26.cloned.1.call-done = bf16[1024,1600]{0,1:T(8,128)(2,1)} async-done(((bf16[128,1600]{0,1:T(8,128)(2,1)}), bf16[1024,1600]{0,1:T(8,128)(2,1)}) %all-gather.26.cloned.1.call-update) | async-done | bytes 3276816 | tf_op jit(solution)/shard_map/all_gather | solution.py:100
  458.8 10.0 fusion.71
  468.8 23.6 %fusion.55 = bf16[1024,1,4,64]{0,3,2,1:T(8,128)(2,1)} fusion(f32[4,1024,1024]{1,2,0:T(8,128)} %fusion.71, f32[4,1024,1024]{1,2,0:T(8,128)} %get-tuple-element.69, f32[4,1024]{1,0:T(4,128)S(1)} %log_add_fusion, bf16[1024,3,4,64]{0,3,2,1:T(8,128)(2,1)} %bitcast.215), kind=kOutput, calls=%fused_computation.52 | convolution fusion | flops 566498304 | bytes 68190208 | tf_op jit(solution)/shard_map/hqk,khd->qhd/dot_general | solution.py:61
  492.4 23.7 %fusion.52 = bf16[1024,1,4,64]{0,3,2,1:T(8,128)(2,1)} fusion(f32[4,1024,1024]{1,2,0:T(8,128)} %fusion.71, f32[4,1024,1024]{1,2,0:T(8,128)} %get-tuple-element.69, f32[4,1024]{1,0:T(4,128)S(1)} %log_add_fusion, bf16[1024,3,4,64]{0,3,2,1:T(8,128)(2,1)} %bitcast.216), kind=kOutput, calls=%fused_computation.51 | convolution fusion | flops 566498304 | bytes 68190208 | tf_op jit(solution)/shard_map/hqk,qhd->khd/dot_general | solution.py:62
  516.1 8.7 fusion.49
  531.1 9.3 fusion.78
  540.4 8.4 fusion.95
  549.0 7.9 fusion.79
  568.8 57.5 %reduce-scatter.13.cloned.1.call-done = f32[128,1600]{0,1:T(8,128)} async-done(((f32[1024,1600]{0,1:T(8,128)}), f32[128,1600]{0,1:T(8,128)}) %reduce-scatter.13.cloned.1.call-update) | async-done | bytes 819216 | tf_op jit(solution)/shard_map/reduce_scatter | solution.py:103
  628.2 64.3 %reduce-scatter.9.cloned.1.call-done = f32[128,1600]{0,1:T(8,128)} async-done(((f32[1024,1600]{0,1:T(8,128)}), f32[128,1600]{0,1:T(8,128)}) %reduce-scatter.9.cloned.1.call-update) | async-done | bytes 819216 | tf_op jit(solution)/shard_map/reduce_scatter | solution.py:103
  695.4 101.2 %reduce-scatter.19.cloned.1.call-done = f32[400,800]{1,0:T(8,128)} async-done(((f32[1600,800]{1,0:T(8,128)}), f32[400,800]{1,0:T(8,128)}) %reduce-scatter.19.cloned.1.call-update) | async-done | bytes 1280016 | tf_op jit(solution)/shard_map/reduce_scatter | solution.py:148
  802.9 84.9 %reduce-scatter.15.cloned.1.call-done = f32[400,768]{1,0:T(8,128)} async-done(((f32[1600,768]{1,0:T(8,128)}), f32[400,768]{1,0:T(8,128)}) %reduce-scatter.15.cloned.1.call-update) | async-done | bytes 1228816 | tf_op jit(solution)/shard_map/reduce_scatter | solution.py:148
  893.8 33.8 %reduce-scatter.17.cloned.1.call-done = f32[256,400]{0,1:T(8,128)} async-done(((f32[256,1600]{0,1:T(8,128)}), f32[256,400]{0,1:T(8,128)}) %reduce-scatter.17.cloned.1.call-update) | async-done | bytes 409616 | tf_op jit(solution)/shard_map/reduce_scatter | solution.py:148
  952.3 75.6 %all-reduce = f32[4,1600]{1,0:T(4,128)S(1)} all-reduce(f32[4,1600]{1,0:T(4,128)S(1)} %pad_maximum_fusion.2), channel_id=10, replica_groups=mesh['fsdp'=4,'ctx'=4,'tp'=2] {'fsdp','ctx'}, use_global_device_ids=true, to_apply=%region_21.22.clone | all-reduce | flops 6400 | bytes 51200
  (183 shorter events, 108.4 us)
Async XLA Ops:
  7.2 28.6 %copy-start = (bf16[400,3200]{1,0:T(8,128)(2,1)S(1)}, bf16[400,3200]{1,0:T(8,128)(2,1)}, u32[]{:S(2)}) copy-start(bf16[400,3200]{1,0:T(8,128)(2,1)} %param.19) | copy-start | bytes 7680004
  7.2 39.3 %all-gather.30.cloned.1.call-start = ((), (), s32[]{:S(2)}) async-start(), calls=%async_computation.26 | async-start | bytes 3686400 | tf_op jit(solution)/shard_map/all_gather | solution.py:100
  9.3 91.3 %all-gather.16.cloned.1.call-start = ((), (), s32[]{:S(2)}) async-start(), calls=%async_computation.12 | async-start | bytes 3072000 | tf_op jit(solution)/shard_map/all_gather | solution.py:91
  11.7 25.3 %copy-start.15 = (s32[1,256]{1,0:T(1,128)S(1)}, s32[1,256]{1,0:T(1,128)}, u32[]{:S(2)}) copy-start(s32[1,256]{1,0:T(1,128)} %param.12) | copy-start | bytes 3076
  11.7 136.3 %all-gather.18.cloned.1.call-start = ((), (), s32[]{:S(2)}) async-start(), calls=%async_computation.13 | async-start | bytes 5990400 | tf_op jit(solution)/shard_map/all_gather | solution.py:94
  35.7 173.8 %all-gather.22.cloned.1.call-start = ((), (), s32[]{:S(2)}) async-start(), calls=%async_computation.15 | async-start | bytes 3584000 | tf_op jit(solution)/shard_map/all_gather | solution.py:96
  37.0 206.9 %all-gather.20.cloned.1.call-start = ((), (), s32[]{:S(2)}) async-start(), calls=%async_computation.14 | async-start | bytes 3686400 | tf_op jit(solution)/shard_map/all_gather | solution.py:100
  45.9 54.7 %copy-start.13 = (f32[1600]{0:T(1024)S(1)}, f32[1600]{0:T(1024)}, u32[]{:S(2)}) copy-start(f32[1600]{0:T(1024)} %param.13) | copy-start | bytes 19204
  46.5 54.1 %copy-start.18 = (f32[1600]{0:T(1024)S(1)}, f32[1600]{0:T(1024)}, u32[]{:S(2)}) copy-start(f32[1600]{0:T(1024)} %param.14) | copy-start | bytes 19204
  106.8 15.5 %copy-start.11 = (bf16[1024,768]{0,1:T(8,128)(2,1)}, bf16[1024,768]{0,1:T(8,128)(2,1)S(1)}, u32[]{:S(2)}) copy-start(bf16[1024,768]{0,1:T(8,128)(2,1)S(1)} %convolution_convert_fusion) | copy-start | bytes 4718596
  130.5 17.5 %copy-start.2 = (bf16[1,128,1600]{1,2,0:T(8,128)(2,1)S(1)}, bf16[1,128,1600]{1,2,0:T(8,128)(2,1)}, u32[]{:S(2)}) copy-start(bf16[1,128,1600]{1,2,0:T(8,128)(2,1)} %get-tuple-element.19) | copy-start | bytes 1228804
  154.2 150.5 %all-gather.24.cloned.1.call-start = ((), (), s32[]{:S(2)}) async-start(), calls=%async_computation.16 | async-start | bytes 3584000 | tf_op jit(solution)/shard_map/all_gather | solution.py:97
  156.6 182.6 %all-gather.32.cloned.1.call-start = ((), (), s32[]{:S(2)}) async-start(), calls=%async_computation.27 | async-start | bytes 3686400 | tf_op jit(solution)/shard_map/all_gather | solution.py:100
  157.5 260.3 %reduce-scatter.11.cloned.1.call-start = ((), (), s32[]{:S(2)}) async-start(), calls=%async_computation.18 | async-start | bytes 7372800 | tf_op jit(solution)/shard_map/reduce_scatter | solution.py:103
  339.2 10.2 copy-start.16
  354.9 100.6 %all-gather.26.cloned.1.call-start = ((), (), s32[]{:S(2)}) async-start(), calls=%async_computation.19 | async-start | bytes 3686400 | tf_op jit(solution)/shard_map/all_gather | solution.py:100
  422.0 139.3 %reduce-scatter.21.cloned.1.call-start = ((), (), s32[]{:S(2)}) async-start(), calls=%async_computation.25 | async-start | bytes 7168000 | tf_op jit(solution)/shard_map/reduce_scatter | solution.py:148
  440.9 185.4 %reduce-scatter.13.cloned.1.call-start = ((), (), s32[]{:S(2)}) async-start(), calls=%async_computation.20 | async-start | bytes 7372800 | tf_op jit(solution)/shard_map/reduce_scatter | solution.py:103
  516.1 10.1 copy-start.17
  530.8 161.7 %reduce-scatter.9.cloned.1.call-start = ((), (), s32[]{:S(2)}) async-start(), calls=%async_computation.17 | async-start | bytes 7372800 | tf_op jit(solution)/shard_map/reduce_scatter | solution.py:103
  540.4 256.2 %reduce-scatter.19.cloned.1.call-start = ((), (), s32[]{:S(2)}) async-start(), calls=%async_computation.24 | async-start | bytes 7168000 | tf_op jit(solution)/shard_map/reduce_scatter | solution.py:148
  548.9 338.9 %reduce-scatter.15.cloned.1.call-start = ((), (), s32[]{:S(2)}) async-start(), calls=%async_computation.22 | async-start | bytes 6144000 | tf_op jit(solution)/shard_map/reduce_scatter | solution.py:148
  556.8 370.7 %reduce-scatter.17.cloned.1.call-start = ((), (), s32[]{:S(2)}) async-start(), calls=%async_computation.23 | async-start | bytes 2048000 | tf_op jit(solution)/shard_map/reduce_scatter | solution.py:148
  561.3 131.2 %copy-start.4 = (f32[128,1600]{0,1:T(8,128)S(1)}, f32[128,1600]{0,1:T(8,128)}, u32[]{:S(2)}) copy-start(f32[128,1600]{0,1:T(8,128)} %reduce-scatter.11.cloned.1.call-done) | copy-start | bytes 2457604
  561.3 131.2 %copy-start.6 = (bf16[1,256,1600]{1,2,0:T(8,128)(2,1)S(1)}, bf16[1,256,1600]{1,2,0:T(8,128)(2,1)}, u32[]{:S(2)}) copy-start(bf16[1,256,1600]{1,2,0:T(8,128)(2,1)} %param.21) | copy-start | bytes 2457604
  564.1 235.1 %all-to-all-start.4 = ((f32[800,4,100]{0,2,1:T(8,128)}), f32[800,4,100]{0,2,1:T(8,128)}, u32[]{:S(2)}, u32[]{:S(2)}) async-start(f32[800,4,100]{0,2,1:T(8,128)} %all_to_all.69), calls=%async_computation.11 | async-start | bytes 2981888 | tf_op jit(solution)/shard_map/all_to_all | solution.py:151
  568.5 462.5 %all-gather.28.cloned.1.call-start = ((), (), s32[]{:S(2)}) async-start(), calls=%async_computation.21 | async-start | bytes 2457600 | tf_op jit(solution)/shard_map/all_gather | solution.py:145
  799.2 90.9 %all-to-all-start.3 = ((f32[4,100,800]{2,1,0:T(8,128)}), f32[4,100,800]{2,1,0:T(8,128)S(1)}, u32[]{:S(2)}, u32[]{:S(2)}) async-start(f32[4,100,800]{2,1,0:T(8,128)} %all_to_all.65), calls=%async_computation.9 | async-start | bytes 2981888 | tf_op jit(solution)/shard_map/all_to_all | solution.py:150
  889.2 44.9 %copy-start.19 = (u32[32]{0:T(128)S(1)}, u32[32]{0:T(128)}, u32[]{:S(2)}) copy-start(u32[32]{0:T(128)} %constant.100) | copy-start | bytes 388
  890.1 39.2 %all-to-all-start.1 = ((bf16[4,100,768]{2,1,0:T(8,128)(2,1)}), bf16[4,100,768]{2,1,0:T(8,128)(2,1)S(1)}, u32[]{:S(2)}, u32[]{:S(2)}) async-start(bf16[4,100,768]{2,1,0:T(8,128)(2,1)} %reshape.173), calls=%async_computation.5 | async-start | bytes 1277952 | tf_op jit(solution)/shard_map/all_to_all | solution.py:154
  929.3 16.2 %all-to-all-start.2 = ((bf16[256,4,100]{0,2,1:T(8,128)(2,1)}), bf16[256,4,100]{0,2,1:T(8,128)(2,1)S(1)}, u32[]{:S(2)}, u32[]{:S(2)}) async-start(bf16[256,4,100]{0,2,1:T(8,128)(2,1)} %all_to_all.62), calls=%async_computation.7 | async-start | bytes 425984 | tf_op jit(solution)/shard_map/all_to_all | solution.py:165
  933.0 98.0 %all-gather.34.cloned.1.call-start = ((), (), s32[]{:S(2)}) async-start(), calls=%async_computation.28 | async-start | bytes 1843200 | tf_op jit(solution)/shard_map/all_gather | solution.py:154
  (10 other events, 48.4 us)
Sparse Core Ops, SparseCore 0:
  10.5 36.0 all-gather.29
  48.7 51.8 all-gather.15
  103.1 44.1 all-gather.17
  149.3 60.2 all-gather.21
  211.8 31.9 all-gather.19
  245.9 58.8 all-gather.23
  307.2 31.9 all-gather.31
  355.0 62.8 reduce-scatter.10
  422.1 33.2 all-gather.25
  457.7 101.7 reduce-scatter.20
  562.9 63.3 reduce-scatter.12
  629.6 62.8 reduce-scatter.8
  694.8 101.7 reduce-scatter.18
  798.8 88.9 reduce-scatter.14
  890.5 36.9 reduce-scatter.16
  929.5 8.4 all-gather.27
  939.9 10.4 all-gather.33
where the time goes:
time: 1060 us; the launch traced here: 1050 us
  waiting for transfers between devices  644 us (61%)
  matrix products  161 us (15%)
  blocking collectives  130 us (12%)
  local copies, waits for them, and re-layouts  43.3 us (4%)
  other arithmetic  32 us (3%)
  starting transfers between devices  26.2 us (2%)
  between operations  15.7 us (1%)
    reduce_scatter x4, waiting for transfers between devices, over_fsdp(): return lax.psum_scatter(v, 'fsdp', scatter_dimension=dim, tiled=True)  220 us
    reduce_scatter x3, waiting for transfers between devices, from_plane(): return lax.psum_scatter(v, PLANE, scatter_dimension=0, tiled=True)  185 us
    all_gather x4, waiting for transfers between devices, to_plane(): return lax.all_gather(v, PLANE, axis=0, tiled=True)  83.9 us
    dot_general x12, matrix products, dot(): lax.dot_general(lhs, rhs, (dims, ((), ())), preferred_element_type=F32)  79.7 us
    unnamed x1, blocking collectives  75.6 us
    all_gather x1, waiting for transfers between devices, local(): lax.all_gather(rows_of(wproj, ctx_i * hidden, hidden), 'fsdp', axis=1, ti...  53.2 us
    all_gather x1, waiting for transfers between devices, local(): lax.all_gather(cols(wfc, ctx_i * hidden, hidden), 'fsdp', axis=0, tiled=T...  52 us
    all_gather x1, waiting for transfers between devices, local(): wq = lax.all_gather(wq, 'fsdp', axis=0, tiled=True)  50.2 us
  transfers between devices with their start and end apart: 21, of which 13 were waited for; matrix products, arithmetic and copies ran while one was open for 18% of the time, Pallas kernels for 0%

commit v1 on v0

--- a/solution.py
+++ b/solution.py
@@ -9,6 +9,22 @@
 BF = jnp.bfloat16
 F32 = jnp.float32
 PLANE = ("ctx", "tp")
+
+
+def _end_islands(block_here, comm_axis):
+    column = [block_here]
+    it = 1
+    axis_n = lax.axis_size(comm_axis)
+    while it < axis_n:
+        carry = lax.ppermute(
+            column[it - 1], comm_axis, [(idx, (idx - 1) % axis_n) for idx in range(axis_n)]
+        )
+        column.append(carry)
+        it += 1
+    mixed_arr = jnp.roll(
+        jnp.concatenate(column, axis=0), lax.axis_index(comm_axis) * block_here.shape[0], axis=0
+    )
+    return mixed_arr
 
 
 def dot(lhs, rhs, dims):
@@ -88,7 +104,7 @@
             return lax.dynamic_slice_in_dim(matrix, start, size, 0)
 
         wq = jnp.concatenate([cols(wqkv, p * H * HD + head0 * HD, width) for p in range(3)], axis=1)
-        wq = lax.all_gather(wq, "fsdp", axis=0, tiled=True)
+        wq = _end_islands(wq, comm_axis="fsdp")
         part = model // members
         wo = lax.all_gather(rows_of(wout, member * part, part), "fsdp", axis=1, tiled=True)
         wo = lax.all_gather(wo, PLANE, axis=0, tiled=True)

time: 1060 us -> 1010 us (0.953)
  waiting for transfers between devices: 644 us -> 578 us
    all_gather x1 -> x0, waiting for transfers between devices: 50.2 us -> none  [local(): wq = lax.all_gather(wq, 'fsdp', axis=0, tiled=True)]
    all_gather x1, waiting for transfers between devices: 52 us -> 6.34 us  [local(): lax.all_gather(cols(wfc, ctx_i * hidden, hidden), 'fsdp', axis=0, tiled=T...]
    ppermute x0 -> x3, waiting for transfers between devices: none -> 23.2 us  [_end_islands(): lax.ppermute(column[it - 1], comm_axis, [(idx, (idx - 1) % axis_n) for id...]
  transfers between devices with their start and end apart: 21 -> 23, of which waited for: 13 -> 13; matrix products, arithmetic and copies ran while one was open for 18% -> 20% of each run, Pallas kernels for 0% -> 0%
where the time goes in v1:
time: 1010 us; the launch traced here: 994 us
  waiting for transfers between devices  578 us (57%)
  matrix products  162 us (16%)
  blocking collectives  125 us (12%)
  local copies, waits for them, and re-layouts  53 us (5%)
  other arithmetic  33 us (3%)
  starting transfers between devices  27 us (3%)
  between operations  15.7 us (2%)
    reduce_scatter x4, waiting for transfers between devices, over_fsdp(): return lax.psum_scatter(v, 'fsdp', scatter_dimension=dim, tiled=True)  220 us
    reduce_scatter x3, waiting for transfers between devices, from_plane(): return lax.psum_scatter(v, PLANE, scatter_dimension=0, tiled=True)  183 us
    all_gather x4, waiting for transfers between devices, to_plane(): return lax.all_gather(v, PLANE, axis=0, tiled=True)  92.7 us
    dot_general x12, matrix products, dot(): lax.dot_general(lhs, rhs, (dims, ((), ())), preferred_element_type=F32)  80.9 us
    unnamed x1, blocking collectives  75.6 us
    all_gather x1, waiting for transfers between devices, local(): lax.all_gather(rows_of(wproj, ctx_i * hidden, hidden), 'fsdp', axis=1, ti...  53.2 us
    dot_general x1, matrix products, attend_back(): jnp.einsum('hqk,qhd->khd', raw, queries, preferred_element_type=F32)  23.7 us
    dot_general x1, matrix products, attend_back(): grad_q = jnp.einsum('hqk,khd->qhd', raw, keys, preferred_element_type=F32)  23.6 us
  transfers between devices with their start and end apart: 23, of which 13 were waited for; matrix products, arithmetic and copies ran while one was open for 20% of the time, Pallas kernels for 0%

profile of v1, /device:TPU:0, one launch (start us, length us, event | category | flops | bytes accessed | tf_op | source)
XLA Modules:
  0.0 994.3 jit_solution(4589829917894144289)
XLA Ops:
  10.5 21.7 %all_gather.44 = bf16[200,1600]{0,1:T(8,128)(2,1)S(1)} all-gather(bf16[200,400]{0,1:T(8,128)(2,1)S(1)} %constant_dynamic-slice_fusion.3), channel_id=1, replica_groups=mesh['fsdp'=4,'ctx'=4,'tp'=2] {'fsdp'}, dimensions={1}, use_global_device_ids=true | all-gather | bytes 800000 | tf_op jit(solution)/shard_map/all_gather | solution.py:109
  37.5 12.0 %collective-permute-done = bf16[400,768]{1,0:T(8,128)(2,1)S(1)} collective-permute-done((bf16[400,768]{1,0:T(8,128)(2,1)S(1)}, bf16[400,768]{1,0:T(8,128)(2,1)S(1)}, u32[]{:S(2)}, u32[]{:S(2)}) %collective-permute-start) | collective-permute-done | bytes 614432 | tf_op jit(solution)/shard_map/ppermute | solution.py:19
  53.8 11.2 %collective-permute-done.1 = bf16[400,768]{1,0:T(8,128)(2,1)} collective-permute-done((bf16[400,768]{1,0:T(8,128)(2,1)S(1)}, bf16[400,768]{1,0:T(8,128)(2,1)}, u32[]{:S(2)}, u32[]{:S(2)}) %collective-permute-start.1) | collective-permute-done | bytes 614432 | tf_op jit(solution)/shard_map/ppermute | solution.py:19
  70.6 8.4 all-gather.1
  99.3 7.4 fusion.100
  106.7 8.1 fusion.4
  114.8 7.5 fusion.55
  122.4 12.8 %all_to_all.78 = bf16[8,128,256]{1,2,0:T(8,128)(2,1)S(1)} all-to-all(bf16[8,128,256]{1,2,0:T(8,128)(2,1)S(1)} %copy.96), channel_id=1, replica_groups=mesh['fsdp'=4,'ctx'=4,'tp'=2] {'ctx','tp'}, dimensions={0} | all-to-all | bytes 1048576 | tf_op jit(solution)/shard_map/all_to_all | solution.py:133
  145.0 6.3 all-gather.19.cloned.1.call-done
  151.3 34.3 %all-gather.17.cloned.1.call-done = bf16[1024,1600]{0,1:T(8,128)(2,1)} async-done(((bf16[128,1600]{0,1:T(8,128)(2,1)}), bf16[1024,1600]{0,1:T(8,128)(2,1)}) %all-gather.17.cloned.1.call-update) | async-done | bytes 3276816 | tf_op jit(solution)/shard_map/all_gather | solution.py:116
  185.7 7.7 fusion.102
  193.3 53.2 %all-gather.21.cloned.1.call-done = bf16[800,1600]{0,1:T(8,128)(2,1)} async-done(((bf16[800,400]{0,1:T(8,128)(2,1)}), bf16[800,1600]{0,1:T(8,128)(2,1)}) %all-gather.21.cloned.1.call-update) | async-done | bytes 2560016 | tf_op jit(solution)/shard_map/all_gather | solution.py:113
  246.5 34.3 %all-gather.29.cloned.1.call-done = bf16[1,1024,1600]{1,2,0:T(8,128)(2,1)} async-done(((bf16[1,128,1600]{1,2,0:T(8,128)(2,1)}), bf16[1,1024,1600]{1,2,0:T(8,128)(2,1)}) %all-gather.29.cloned.1.call-update) | async-done | bytes 3276816 | tf_op jit(solution)/shard_map/all_gather | solution.py:116
  280.9 9.0 fusion.31
  291.0 5.5 fusion.105
  296.6 63.0 %reduce-scatter.11.cloned.1.call-done = f32[128,1600]{0,1:T(8,128)} async-done(((f32[1024,1600]{0,1:T(8,128)}), f32[128,1600]{0,1:T(8,128)}) %reduce-scatter.11.cloned.1.call-update) | async-done | bytes 819216 | tf_op jit(solution)/shard_map/reduce_scatter | solution.py:119
  363.9 9.1 fusion.32
  373.1 24.0 %all-gather.23.cloned.1.call-done = bf16[1024,1600]{0,1:T(8,128)(2,1)} async-done(((bf16[128,1600]{0,1:T(8,128)(2,1)}), bf16[1024,1600]{0,1:T(8,128)(2,1)}) %all-gather.23.cloned.1.call-update) | async-done | bytes 3276816 | tf_op jit(solution)/shard_map/all_gather | solution.py:116
  400.4 10.0 %fusion.78 = f32[4,1024,1024]{1,2,0:T(8,128)} fusion(bf16[1024,4,64]{0,2,1:T(8,128)(2,1)S(1)} %bitcast.192, bf16[1024,3,4,64]{0,3,2,1:T(8,128)(2,1)} %bitcast.212), kind=kOutput, calls=%fused_computation.85 | convolution fusion | flops 536870912 | bytes 17825792 | tf_op jit(solution)/shard_map/qhd,khd->hqk/dot_general | solution.py:74
  410.5 23.6 %fusion.62 = bf16[1024,1,4,64]{0,3,2,1:T(8,128)(2,1)} fusion(f32[4,1024,1024]{1,2,0:T(8,128)} %fusion.78, f32[4,1024,1024]{1,2,0:T(8,128)} %get-tuple-element.71, f32[4,1024]{1,0:T(4,128)S(1)} %log_add_fusion, bf16[1024,3,4,64]{0,3,2,1:T(8,128)(2,1)} %bitcast.213), kind=kOutput, calls=%fused_computation.56 | convolution fusion | flops 566498304 | bytes 68190208 | tf_op jit(solution)/shard_map/hqk,khd->qhd/dot_general | solution.py:77
  434.0 23.7 %fusion.59 = bf16[1024,1,4,64]{0,3,2,1:T(8,128)(2,1)} fusion(f32[4,1024,1024]{1,2,0:T(8,128)} %fusion.78, f32[4,1024,1024]{1,2,0:T(8,128)} %get-tuple-element.71, f32[4,1024]{1,0:T(4,128)S(1)} %log_add_fusion, bf16[1024,3,4,64]{0,3,2,1:T(8,128)(2,1)} %bitcast.214), kind=kOutput, calls=%fused_computation.55 | convolution fusion | flops 566498304 | bytes 68190208 | tf_op jit(solution)/shard_map/hqk,qhd->khd/dot_general | solution.py:78
  457.8 8.7 fusion.56
  467.8 6.4 fusion.38
  474.5 9.3 fusion.87
  483.8 8.5 fusion.104
  492.4 8.0 fusion.88
  512.5 55.5 %reduce-scatter.13.cloned.1.call-done = f32[128,1600]{0,1:T(8,128)} async-done(((f32[1024,1600]{0,1:T(8,128)}), f32[128,1600]{0,1:T(8,128)}) %reduce-scatter.13.cloned.1.call-update) | async-done | bytes 819216 | tf_op jit(solution)/shard_map/reduce_scatter | solution.py:119
  569.9 64.4 %reduce-scatter.9.cloned.1.call-done = f32[128,1600]{0,1:T(8,128)} async-done(((f32[1024,1600]{0,1:T(8,128)}), f32[128,1600]{0,1:T(8,128)}) %reduce-scatter.9.cloned.1.call-update) | async-done | bytes 819216 | tf_op jit(solution)/shard_map/reduce_scatter | solution.py:119
  637.2 101.0 %reduce-scatter.19.cloned.1.call-done = f32[400,800]{1,0:T(8,128)} async-done(((f32[1600,800]{1,0:T(8,128)}), f32[400,800]{1,0:T(8,128)}) %reduce-scatter.19.cloned.1.call-update) | async-done | bytes 1280016 | tf_op jit(solution)/shard_map/reduce_scatter | solution.py:164
  744.6 85.1 %reduce-scatter.15.cloned.1.call-done = f32[400,768]{1,0:T(8,128)} async-done(((f32[1600,768]{1,0:T(8,128)}), f32[400,768]{1,0:T(8,128)}) %reduce-scatter.15.cloned.1.call-update) | async-done | bytes 1228816 | tf_op jit(solution)/shard_map/reduce_scatter | solution.py:164
  835.6 33.8 %reduce-scatter.17.cloned.1.call-done = f32[256,400]{0,1:T(8,128)} async-done(((f32[256,1600]{0,1:T(8,128)}), f32[256,400]{0,1:T(8,128)}) %reduce-scatter.17.cloned.1.call-update) | async-done | bytes 409616 | tf_op jit(solution)/shard_map/reduce_scatter | solution.py:164
  894.1 75.6 %all-reduce = f32[4,1600]{1,0:T(4,128)S(1)} all-reduce(f32[4,1600]{1,0:T(4,128)S(1)} %pad_maximum_fusion.2), channel_id=10, replica_groups=mesh['fsdp'=4,'ctx'=4,'tp'=2] {'fsdp','ctx'}, use_global_device_ids=true, to_apply=%region_21.22.clone | all-reduce | flops 6400 | bytes 51200
  (199 shorter events, 129.7 us)
Async XLA Ops:
  7.2 62.2 %copy-start = (bf16[400,3200]{1,0:T(8,128)(2,1)S(1)}, bf16[400,3200]{1,0:T(8,128)(2,1)}, u32[]{:S(2)}) copy-start(bf16[400,3200]{1,0:T(8,128)(2,1)} %param.19) | copy-start | bytes 7680004
  7.2 82.9 %all-gather.27.cloned.1.call-start = ((), (), s32[]{:S(2)}) async-start(), calls=%async_computation.25 | async-start | bytes 3686400 | tf_op jit(solution)/shard_map/all_gather | solution.py:116
  9.3 126.1 %all-gather.15.cloned.1.call-start = ((), (), s32[]{:S(2)}) async-start(), calls=%async_computation.12 | async-start | bytes 5990400 | tf_op jit(solution)/shard_map/all_gather | solution.py:110
  33.3 37.3 %copy-start.19 = (s32[1,256]{1,0:T(1,128)S(1)}, s32[1,256]{1,0:T(1,128)}, u32[]{:S(2)}) copy-start(s32[1,256]{1,0:T(1,128)} %param.12) | copy-start | bytes 3076
  33.3 118.0 %all-gather.19.cloned.1.call-start = ((), (), s32[]{:S(2)}) async-start(), calls=%async_computation.14 | async-start | bytes 3584000 | tf_op jit(solution)/shard_map/all_gather | solution.py:112
  34.9 14.6 %copy-start.7 = (bf16[400,256]{1,0:T(8,128)(2,1)}, bf16[400,256]{1,0:T(8,128)(2,1)S(1)}, u32[]{:S(2)}) copy-start(bf16[400,256]{1,0:T(8,128)(2,1)S(1)} %get-tuple-element.21) | copy-start | bytes 614404
  34.9 14.6 %copy-start.9 = (bf16[400,256]{1,0:T(8,128)(2,1)}, bf16[400,256]{1,0:T(8,128)(2,1)S(1)}, u32[]{:S(2)}) copy-start(bf16[400,256]{1,0:T(8,128)(2,1)S(1)} %get-tuple-element.22) | copy-start | bytes 614404
  35.8 13.7 %collective-permute-start = (bf16[400,768]{1,0:T(8,128)(2,1)S(1)}, bf16[400,768]{1,0:T(8,128)(2,1)S(1)}, u32[]{:S(2)}, u32[]{:S(2)}) collective-permute-start(bf16[400,768]{1,0:T(8,128)(2,1)S(1)} %get-tuple-element.33), channel_id=1, source_target_pairs={{0,24},{8,0},{16,8},{24,16},{1,25},{9,1},{17,9},{25,17},{2,26},{10... | collective-permute-start | bytes 1843208 | tf_op jit(solution)/shard_map/ppermute | solution.py:19
  49.5 15.4 %collective-permute-start.1 = (bf16[400,768]{1,0:T(8,128)(2,1)S(1)}, bf16[400,768]{1,0:T(8,128)(2,1)}, u32[]{:S(2)}, u32[]{:S(2)}) collective-permute-start(bf16[400,768]{1,0:T(8,128)(2,1)S(1)} %collective-permute-done), channel_id=1, source_target_pairs={{0,24},{8,0},{16,8},{24,16},{1,25},{9,1},{17,9},{25,17},{2,26},{10... | collective-permute-start | bytes 1843208 | tf_op jit(solution)/shard_map/ppermute | solution.py:19
  64.9 17.5 %collective-permute-start.2 = (bf16[400,768]{1,0:T(8,128)(2,1)}, bf16[400,768]{1,0:T(8,128)(2,1)}, u32[]{:S(2)}, u32[]{:S(2)}) collective-permute-start(bf16[400,768]{1,0:T(8,128)(2,1)} %collective-permute-done.1), channel_id=1, source_target_pairs={{0,24},{8,0},{16,8},{24,16},{1,25},{9,1},{17,9},{25,17},{2,26},{10... | collective-permute-start | bytes 1843208 | tf_op jit(solution)/shard_map/ppermute | solution.py:19
  70.5 13.9 %copy-start.10 = (bf16[400,256]{1,0:T(8,128)(2,1)S(1)}, bf16[400,256]{1,0:T(8,128)(2,1)}, u32[]{:S(2)}) copy-start(bf16[400,256]{1,0:T(8,128)(2,1)} %copy-done.9) | copy-start | bytes 614404
  70.5 115.1 %all-gather.17.cloned.1.call-start = ((), (), s32[]{:S(2)}) async-start(), calls=%async_computation.13 | async-start | bytes 3686400 | tf_op jit(solution)/shard_map/all_gather | solution.py:116
  99.3 15.5 %copy-start.15 = (bf16[1024,768]{0,1:T(8,128)(2,1)}, bf16[1024,768]{0,1:T(8,128)(2,1)S(1)}, u32[]{:S(2)}) copy-start(bf16[1024,768]{0,1:T(8,128)(2,1)S(1)} %fusion.42) | copy-start | bytes 4718596
  141.7 104.8 %all-gather.21.cloned.1.call-start = ((), (), s32[]{:S(2)}) async-start(), calls=%async_computation.15 | async-start | bytes 3584000 | tf_op jit(solution)/shard_map/all_gather | solution.py:113
  144.1 136.8 %all-gather.29.cloned.1.call-start = ((), (), s32[]{:S(2)}) async-start(), calls=%async_computation.26 | async-start | bytes 3686400 | tf_op jit(solution)/shard_map/all_gather | solution.py:116
  145.0 214.5 %reduce-scatter.11.cloned.1.call-start = ((), (), s32[]{:S(2)}) async-start(), calls=%async_computation.17 | async-start | bytes 7372800 | tf_op jit(solution)/shard_map/reduce_scatter | solution.py:119
  296.5 100.6 %all-gather.23.cloned.1.call-start = ((), (), s32[]{:S(2)}) async-start(), calls=%async_computation.18 | async-start | bytes 3686400 | tf_op jit(solution)/shard_map/all_gather | solution.py:116
  363.7 141.3 %reduce-scatter.21.cloned.1.call-start = ((), (), s32[]{:S(2)}) async-start(), calls=%async_computation.24 | async-start | bytes 7168000 | tf_op jit(solution)/shard_map/reduce_scatter | solution.py:164
  373.0 195.0 %reduce-scatter.13.cloned.1.call-start = ((), (), s32[]{:S(2)}) async-start(), calls=%async_computation.19 | async-start | bytes 7372800 | tf_op jit(solution)/shard_map/reduce_scatter | solution.py:119
  474.2 160.1 %reduce-scatter.9.cloned.1.call-start = ((), (), s32[]{:S(2)}) async-start(), calls=%async_computation.16 | async-start | bytes 7372800 | tf_op jit(solution)/shard_map/reduce_scatter | solution.py:119
  483.8 254.5 %reduce-scatter.19.cloned.1.call-start = ((), (), s32[]{:S(2)}) async-start(), calls=%async_computation.23 | async-start | bytes 7168000 | tf_op jit(solution)/shard_map/reduce_scatter | solution.py:164
  492.3 337.3 %reduce-scatter.15.cloned.1.call-start = ((), (), s32[]{:S(2)}) async-start(), calls=%async_computation.21 | async-start | bytes 6144000 | tf_op jit(solution)/shard_map/reduce_scatter | solution.py:164
  500.4 369.0 %reduce-scatter.17.cloned.1.call-start = ((), (), s32[]{:S(2)}) async-start(), calls=%async_computation.22 | async-start | bytes 2048000 | tf_op jit(solution)/shard_map/reduce_scatter | solution.py:164
  504.9 129.4 %copy-start.4 = (f32[128,1600]{0,1:T(8,128)S(1)}, f32[128,1600]{0,1:T(8,128)}, u32[]{:S(2)}) copy-start(f32[128,1600]{0,1:T(8,128)} %reduce-scatter.11.cloned.1.call-done) | copy-start | bytes 2457604
  504.9 129.4 %copy-start.6 = (bf16[1,256,1600]{1,2,0:T(8,128)(2,1)S(1)}, bf16[1,256,1600]{1,2,0:T(8,128)(2,1)}, u32[]{:S(2)}) copy-start(bf16[1,256,1600]{1,2,0:T(8,128)(2,1)} %param.21) | copy-start | bytes 2457604
  507.8 233.2 %all-to-all-start.4 = ((f32[800,4,100]{0,2,1:T(8,128)}), f32[800,4,100]{0,2,1:T(8,128)}, u32[]{:S(2)}, u32[]{:S(2)}) async-start(f32[800,4,100]{0,2,1:T(8,128)} %all_to_all.69), calls=%async_computation.11 | async-start | bytes 2981888 | tf_op jit(solution)/shard_map/all_to_all | solution.py:167
  512.2 460.6 %all-gather.25.cloned.1.call-start = ((), (), s32[]{:S(2)}) async-start(), calls=%async_computation.20 | async-start | bytes 2457600 | tf_op jit(solution)/shard_map/all_gather | solution.py:161
  740.9 91.0 %all-to-all-start.3 = ((f32[4,100,800]{2,1,0:T(8,128)}), f32[4,100,800]{2,1,0:T(8,128)S(1)}, u32[]{:S(2)}, u32[]{:S(2)}) async-start(f32[4,100,800]{2,1,0:T(8,128)} %all_to_all.65), calls=%async_computation.9 | async-start | bytes 2981888 | tf_op jit(solution)/shard_map/all_to_all | solution.py:166
  831.0 44.9 %copy-start.22 = (u32[32]{0:T(128)S(1)}, u32[32]{0:T(128)}, u32[]{:S(2)}) copy-start(u32[32]{0:T(128)} %constant.121) | copy-start | bytes 388
  832.0 39.2 %all-to-all-start.1 = ((bf16[4,100,768]{2,1,0:T(8,128)(2,1)}), bf16[4,100,768]{2,1,0:T(8,128)(2,1)S(1)}, u32[]{:S(2)}, u32[]{:S(2)}) async-start(bf16[4,100,768]{2,1,0:T(8,128)(2,1)} %reshape.173), calls=%async_computation.5 | async-start | bytes 1277952 | tf_op jit(solution)/shard_map/all_to_all | solution.py:170
  871.1 16.2 %all-to-all-start.2 = ((bf16[256,4,100]{0,2,1:T(8,128)(2,1)}), bf16[256,4,100]{0,2,1:T(8,128)(2,1)S(1)}, u32[]{:S(2)}, u32[]{:S(2)}) async-start(bf16[256,4,100]{0,2,1:T(8,128)(2,1)} %all_to_all.62), calls=%async_computation.7 | async-start | bytes 425984 | tf_op jit(solution)/shard_map/all_to_all | solution.py:181
  874.8 98.0 %all-gather.31.cloned.1.call-start = ((), (), s32[]{:S(2)}) async-start(), calls=%async_computation.27 | async-start | bytes 1843200 | tf_op jit(solution)/shard_map/all_gather | solution.py:170
  (15 other events, 93.3 us)
Sparse Core Ops, SparseCore 0:
  10.5 36.0 all-gather.26
  49.0 41.3 all-gather.14
  92.5 58.8 all-gather.18
  153.6 31.9 all-gather.16
  187.7 58.8 all-gather.20
  248.8 31.9 all-gather.28
  296.6 62.8 reduce-scatter.10
  363.8 33.2 all-gather.22
  399.5 101.7 reduce-scatter.20
  504.5 63.4 reduce-scatter.12
  571.5 62.8 reduce-scatter.8
  636.5 101.7 reduce-scatter.18
  740.6 88.9 reduce-scatter.14
  832.4 36.9 reduce-scatter.16
  871.4 8.4 all-gather.24
  881.8 10.4 all-gather.30
